TPU v7x, 32 devices: a whole 2x2x4 slice. The times are simulated.
32 devices in a mesh: seq: 8 (over z, x), head: 4 (over y, core).
Axes of the slice: x: 2, y: 2, z: 4, core: 2. Of those that a mesh axis runs over, the one named last changes fastest.
Arguments:
- queries: bfloat16 [1024, 3072], P('seq', 'head'), may hold values from -8 to 8
- latents: bfloat16 [1024, 576], P('seq'), may hold values from -8 to 8
- key_up: bfloat16 [512, 2048], P(None, 'head'), may hold values from -0.25 to 0.25
- value_up: bfloat16 [512, 2048], P(None, 'head'), may hold values from -0.25 to 0.25
- out_grad: bfloat16 [1024, 2048], P('seq', 'head'), may hold values from -48 to 48
- positions: int32 [1024], P('seq'), may hold values from 0 to 1023, as said below
Outputs:
- query_grad: bfloat16 [1024, 3072], P('seq', 'head')
- latent_grad: float32 [1024, 576], P('seq')
- key_up_grad: float32 [512, 2048], P(None, 'head')
- value_up_grad: float32 [512, 2048], P(None, 'head')
Inputs may be any that keep to these rules, and one draw needn't show every extreme that they name: Every position from 0 to 1023 occurs once; positions come in stripes of 128 consecutive positions in ascending order, each stripe whole within the rows of one device.
All inputs are finite; a program needn't handle non-finite values.
Results may differ from a plain program's by a relative error of at most 0.0084.
Values may be sent and summed in bfloat16 or wider, within the bound.
A program may use at most 64 MiB of HBM per device.

v0:
```python
import math

import jax
import jax.numpy as jnp
from jax import lax
from jax.sharding import PartitionSpec as P

D_LAT = 512
D_ROPE = 64
D_NOPE = 128
D_V = 128


NEG = -1e30


def shifted(value, axis, steps):
    count = lax.axis_size(axis)
    pairs = [(source, (source + steps) % count) for source in range(count)]
    return lax.ppermute(value, axis, pairs)


def up_project(block, key_up, value_up):
    compressed = block[:, :D_LAT]
    key_nope = jnp.dot(compressed, key_up, preferred_element_type=jnp.float32).astype(jnp.bfloat16)
    values = jnp.dot(compressed, value_up, preferred_element_type=jnp.float32).astype(jnp.bfloat16)
    return (key_nope, block[:, D_LAT:], values)


def split_heads(queries, out_grad, key_nope, values):
    heads = key_nope.shape[1] // D_NOPE
    shaped = queries.reshape(queries.shape[0], heads, D_NOPE + D_ROPE)
    grads = out_grad.reshape(out_grad.shape[0], heads, D_V)
    key3 = key_nope.reshape(key_nope.shape[0], heads, D_NOPE)
    value3 = values.reshape(values.shape[0], heads, D_V)
    return (shaped[:, :, :D_NOPE], shaped[:, :, D_NOPE:], grads, key3, value3)


def scores_of(q_nope, q_rope, key3, rope_keys, query_pos, key_pos):
    scale = 1.0 / math.sqrt(D_NOPE + D_ROPE)
    raw = jnp.einsum("bhd,khd->hbk", q_nope, key3, preferred_element_type=jnp.float32)
    raw = raw + jnp.einsum("bhd,kd->hbk", q_rope, rope_keys, preferred_element_type=jnp.float32)
    visible = (key_pos[None, :] <= query_pos[:, None])[None]
    return (raw * scale, visible)


def forward_update(stats, queries, out_grad, query_pos, key_nope, rope_keys, values, key_pos):
    top, total, weighted = stats
    q_nope, q_rope, grads, key3, value3 = split_heads(queries, out_grad, key_nope, values)
    scores, visible = scores_of(q_nope, q_rope, key3, rope_keys, query_pos, key_pos)
    dprobs = jnp.einsum("bhd,khd->hbk", grads, value3, preferred_element_type=jnp.float32)
    masked = jnp.where(visible, scores, NEG)
    new_top = jnp.maximum(top, jnp.max(masked, axis=2))
    weights = jnp.exp(jnp.where(visible, scores - new_top[:, :, None], NEG))
    fade = jnp.exp(top - new_top)
    total = total * fade + jnp.sum(weights, axis=2)
    weighted = weighted * fade + jnp.sum(weights * dprobs, axis=2)
    return (new_top, total, weighted)


def backward_terms(queries, out_grad, query_pos, lse, delta, key_nope, rope_keys, values, key_pos):
    scale = 1.0 / math.sqrt(D_NOPE + D_ROPE)
    q_nope, q_rope, grads, key3, value3 = split_heads(queries, out_grad, key_nope, values)
    scores, visible = scores_of(q_nope, q_rope, key3, rope_keys, query_pos, key_pos)
    probs = jnp.exp(jnp.where(visible, scores - lse[:, :, None], NEG))
    dprobs = jnp.einsum("bhd,khd->hbk", grads, value3, preferred_element_type=jnp.float32)
    dscore = (probs * (dprobs - delta[:, :, None]) * scale).astype(jnp.bfloat16)
    probs16 = probs.astype(jnp.bfloat16)
    grad_nope = jnp.einsum("hbk,khd->bhd", dscore, key3, preferred_element_type=jnp.float32)
    grad_rope = jnp.einsum("hbk,kd->bhd", dscore, rope_keys, preferred_element_type=jnp.float32)
    q_grad = jnp.concatenate([grad_nope, grad_rope], axis=2).reshape(queries.shape[0], -1)
    key_part = jnp.einsum("hbk,bhd->khd", dscore, q_nope, preferred_element_type=jnp.float32)
    value_part = jnp.einsum("hbk,bhd->khd", probs16, grads, preferred_element_type=jnp.float32)
    rope_part = jnp.einsum("hbk,bhd->kd", dscore, q_rope, preferred_element_type=jnp.float32)
    key_rows = key3.shape[0]
    part = jnp.concatenate(
        [key_part.reshape(key_rows, -1), value_part.reshape(key_rows, -1), rope_part], axis=1
    )
    return (q_grad, part)


def shards(queries, latents, key_up, value_up, out_grad, positions):
    rows = queries.shape[0]
    heads = key_up.shape[1] // D_NOPE
    qcols = queries.shape[1]
    nseq = lax.axis_size("seq")
    here = lax.axis_index("seq")
    every_pos = lax.all_gather(positions, "seq", axis=0, tiled=True)
    part_width = heads * (D_NOPE + D_V) + D_ROPE

    def owner_start(step):
        return (here - step) % nseq * rows

    def owner_pos(step):
        return lax.dynamic_slice_in_dim(every_pos, owner_start(step), rows, 0)

    start_stats = (
        jnp.full((heads, rows), NEG, jnp.float32),
        jnp.zeros((heads, rows), jnp.float32),
        jnp.zeros((heads, rows), jnp.float32),
    )
    zero_grads = jnp.zeros((rows, part_width), jnp.float32)
    zero_query = jnp.zeros((rows, qcols), jnp.float32)

    def fold_block(stats, block, start):
        key_nope, rope_keys, values = up_project(block, key_up, value_up)
        key_pos = lax.dynamic_slice_in_dim(every_pos, start, block.shape[0], 0)
        return forward_update(
            stats, queries, out_grad, positions, key_nope, rope_keys, values, key_pos
        )

    def grad_block(block, grads, q_acc, step, lse, delta):
        key_nope, rope_keys, values = up_project(block, key_up, value_up)
        q_grad, part = backward_terms(
            queries, out_grad, positions, lse, delta, key_nope, rope_keys, values, owner_pos(step)
        )
        return (grads + part, q_acc + q_grad)

    gathered = lax.all_gather(latents, "seq", axis=0, tiled=True)
    count = gathered.shape[0]
    width = math.gcd(count, 512)

    def turn(index, carry):
        block = lax.dynamic_slice_in_dim(gathered, index * width, width, 0)
        return fold_block(carry, block, index * width)

    top, total, weighted = lax.fori_loop(0, count // width, turn, start_stats)
    lse = top + jnp.log(total)
    delta = weighted / total

    def kept_turn(step, carry):
        grads, q_acc = carry
        block = lax.dynamic_slice_in_dim(gathered, owner_start(step), rows, 0)
        grads, q_acc = grad_block(block, grads, q_acc, step, lse, delta)
        grads = shifted(grads, "seq", 1)
        return (grads, q_acc)

    grads, q_acc = lax.fori_loop(0, nseq - 1, kept_turn, (zero_grads, zero_query))
    last_block = lax.dynamic_slice_in_dim(gathered, owner_start(nseq - 1), rows, 0)
    grads, q_acc = grad_block(last_block, grads, q_acc, nseq - 1, lse, delta)
    key_grads = shifted(grads, "seq", 1)
    split_one = heads * D_NOPE
    split_two = split_one + heads * D_V
    key_grad = key_grads[:, :split_one]
    value_grad = key_grads[:, split_one:split_two]
    high = lax.Precision.HIGHEST
    key_up32 = key_up.astype(jnp.float32)
    value_up32 = value_up.astype(jnp.float32)
    inner = (((1,), (1,)), ((), ()))
    folded = lax.dot_general(key_grad, key_up32, inner, precision=high)
    folded = folded + lax.dot_general(value_grad, value_up32, inner, precision=high)
    latent_part = jnp.concatenate([folded, key_grads[:, split_two:]], axis=1)
    latent_grad = lax.psum(latent_part, "head")
    compressed = latents[:, :D_LAT].astype(jnp.float32)
    outer = (((0,), (0,)), ((), ()))
    key_term = lax.dot_general(compressed, key_grad, outer, precision=high)
    value_term = lax.dot_general(compressed, value_grad, outer, precision=high)
    key_up_grad, value_up_grad = lax.psum((key_term, value_term), "seq")
    return (q_acc.astype(jnp.bfloat16), latent_grad, key_up_grad, value_up_grad)


def solution(mesh):
    in_specs = (
        P("seq", "head"),
        P("seq", None),
        P(None, "head"),
        P(None, "head"),
        P("seq", "head"),
        P("seq"),
    )
    out_specs = (P("seq", "head"), P("seq", None), P(None, "head"), P(None, "head"))
    return jax.shard_map(shards, mesh=mesh, in_specs=in_specs, out_specs=out_specs, check_vma=False)
```

profile of v0, /device:TPU:17, one launch (start us, length us, event | category | flops | bytes accessed | tf_op | source)
XLA Modules:
  0.0 361.8 jit_solution(10623151957692037776)
XLA Ops:
  10.2 11.9 %all-gather = s32[8,1,128]{2,1,0:T(1,128)S(1)} all-gather(s32[1,1,128]{2,1,0:T(1,128)} %bitcast.257), channel_id=1, replica_groups=mesh['seq'=8,'head'=4] {'seq'}, dimensions={0}, use_global_device_ids=true | all-gather | bytes 4608 | tf_op jit(solution)/shard_map/all_gather | solution.py:88
  22.9 27.0 %all-gather.3.cloned.1.call-done = bf16[1024,576]{0,1:T(8,128)(2,1)} async-done(((bf16[128,576]{0,1:T(8,128)(2,1)}), bf16[1024,576]{0,1:T(8,128)(2,1)}) %all-gather.3.cloned.1.call-update) | async-done | bytes 1179664 | tf_op jit(solution)/shard_map/all_gather | solution.py:119
  49.9 1.4 convolution_convert_fusion.5
  51.5 7.6 %while.36 = (s32[]{:T(128)}, f32[4,128]{1,0:T(4,128)S(1)}, f32[4,128]{1,0:T(4,128)S(1)}, f32[4,128]{1,0:T(4,128)S(1)}, s32[1024]{0:T(1024)S(1)}, /*index=5*/s32[...) while((s32[]{:T(128)}, f32[4,128]{1,0:T(4,128)S(1)}, ...), condition=%wide.region_4.5_spmd.clone, body=%wide.region_0.4_spmd.clone.sunk | while | flops 708120064 | bytes 14854930 | solution.py:127
  51.7 1.6 convolution_convert_fusion.10
  55.5 1.6 convolution_convert_fusion.10
  60.5 1.2 fusion.47
  63.0 118.3 %while.37 = (s32[]{:T(128)}, f32[128,1088]{0,1:T(8,128)S(1)}, f32[128,768]{0,1:T(8,128)S(1)}, s32[]{:T(128)}, s32[1024]{0:T(1024)S(1)}, /*index=5*/s32[128]{0:T(...) while((s32[]{:T(128)}, f32[128,1088]{0,1:T(8,128)S(1)}, ...), condition=%wide.region_6.7_spmd.clone, body=%wide.region_5.6_spmd.clone.sunk | while | flops 244719632 | bytes 11737526 | solution.py:138
  63.1 1.2 fusion.162
  64.3 1.2 convolution_convert_fusion.11
  70.1 12.4 %collective-permute-done = f32[128,1088]{0,1:T(8,128)S(1)} collective-permute-done((f32[128,1088]{0,1:T(8,128)}, f32[128,1088]{0,1:T(8,128)S(1)}, u32[]{:S(2)}, u32[]{:S(2)}) %collective-permute-start) | collective-permute-done | bytes 557088 | tf_op jit(solution)/shard_map/while/body/eval_jaxpr/ppermute | solution.py:20
  83.7 1.2 convolution_convert_fusion.11
  89.1 11.9 %collective-permute-done = f32[128,1088]{0,1:T(8,128)S(1)} collective-permute-done((f32[128,1088]{0,1:T(8,128)}, f32[128,1088]{0,1:T(8,128)S(1)}, u32[]{:S(2)}, u32[]{:S(2)}) %collective-permute-start) | collective-permute-done | bytes 557088 | tf_op jit(solution)/shard_map/while/body/eval_jaxpr/ppermute | solution.py:20
  102.2 1.2 convolution_convert_fusion.11
  107.6 11.0 %collective-permute-done = f32[128,1088]{0,1:T(8,128)S(1)} collective-permute-done((f32[128,1088]{0,1:T(8,128)}, f32[128,1088]{0,1:T(8,128)S(1)}, u32[]{:S(2)}, u32[]{:S(2)}) %collective-permute-start) | collective-permute-done | bytes 557088 | tf_op jit(solution)/shard_map/while/body/eval_jaxpr/ppermute | solution.py:20
  119.9 1.2 convolution_convert_fusion.11
  125.3 10.2 %collective-permute-done = f32[128,1088]{0,1:T(8,128)S(1)} collective-permute-done((f32[128,1088]{0,1:T(8,128)}, f32[128,1088]{0,1:T(8,128)S(1)}, u32[]{:S(2)}, u32[]{:S(2)}) %collective-permute-start) | collective-permute-done | bytes 557088 | tf_op jit(solution)/shard_map/while/body/eval_jaxpr/ppermute | solution.py:20
  136.7 1.2 convolution_convert_fusion.11
  142.1 9.3 %collective-permute-done = f32[128,1088]{0,1:T(8,128)S(1)} collective-permute-done((f32[128,1088]{0,1:T(8,128)}, f32[128,1088]{0,1:T(8,128)S(1)}, u32[]{:S(2)}, u32[]{:S(2)}) %collective-permute-start) | collective-permute-done | bytes 557088 | tf_op jit(solution)/shard_map/while/body/eval_jaxpr/ppermute | solution.py:20
  152.6 1.2 convolution_convert_fusion.11
  158.0 8.3 %collective-permute-done = f32[128,1088]{0,1:T(8,128)S(1)} collective-permute-done((f32[128,1088]{0,1:T(8,128)}, f32[128,1088]{0,1:T(8,128)S(1)}, u32[]{:S(2)}, u32[]{:S(2)}) %collective-permute-start) | collective-permute-done | bytes 557088 | tf_op jit(solution)/shard_map/while/body/eval_jaxpr/ppermute | solution.py:20
  166.4 1.2 fusion.162
  167.6 1.2 convolution_convert_fusion.11
  173.0 8.3 %collective-permute-done = f32[128,1088]{0,1:T(8,128)S(1)} collective-permute-done((f32[128,1088]{0,1:T(8,128)}, f32[128,1088]{0,1:T(8,128)S(1)}, u32[]{:S(2)}, u32[]{:S(2)}) %collective-permute-start) | collective-permute-done | bytes 557088 | tf_op jit(solution)/shard_map/while/body/eval_jaxpr/ppermute | solution.py:20
  182.4 12.2 %collective-permute-done.1 = f32[128,1088]{0,1:T(8,128)S(1)} collective-permute-done((f32[128,1088]{0,1:T(8,128)S(1)}, f32[128,1088]{0,1:T(8,128)S(1)}, u32[]{:S(2)}, u32[]{:S(2)}) %collective-permute-start.1) | collective-permute-done | bytes 557088 | tf_op jit(solution)/shard_map/ppermute | solution.py:20
  196.9 1.5 convolution_bitcast_fusion.9
  198.5 1.6 convolution_bitcast_fusion.8
  202.2 42.3 %all-reduce.4.cloned.1.call-done = f32[128,576]{1,0:T(8,128)} async-done(((f32[128,576]{1,0:T(8,128)}), f32[128,576]{1,0:T(8,128)}) %all-reduce.4.cloned.1.call-update) | async-done | bytes 294928 | tf_op jit(solution)/shard_map/psum | solution.py:153
  244.5 1.8 copy.123
  246.4 105.0 %all-reduce.6.cloned.1.call-done = (f32[512,512]{0,1:T(8,128)}, f32[512,512]{0,1:T(8,128)}) async-done(((f32[512,512]{0,1:T(8,128)}, f32[512,512]{0,1:T(8,128)}), (f32[512,512]{0,1:T(8,128)}, f32[512,512]{0,1:T(8,128)})) %all-reduce.6.cloned.1.call-update) | async-done | bytes 2097168 | tf_op jit(solution)/shard_map/psum | solution.py:158
  351.3 2.6 copy.124
  354.0 1.3 copy.125
  (182 shorter events, 52.0 us)
Async XLA Ops:
  7.2 44.3 %copy-start.5 = (bf16[128,512]{1,0:T(8,128)(2,1)S(1)}, bf16[128,512]{1,0:T(8,128)(2,1)}, u32[]{:S(2)}) copy-start(bf16[128,512]{1,0:T(8,128)(2,1)} %param.14) | copy-start | bytes 393220
  7.2 44.3 %copy-start.6 = (s32[128]{0:T(128)S(1)}, s32[128]{0:T(128)}, u32[]{:S(2)}) copy-start(s32[128]{0:T(128)} %param.15) | copy-start | bytes 1540
  7.2 44.3 %copy-start.1 = (bf16[512,512]{1,0:T(8,128)(2,1)S(1)}, bf16[512,512]{1,0:T(8,128)(2,1)}, u32[]{:S(2)}) copy-start(bf16[512,512]{1,0:T(8,128)(2,1)} %param.12) | copy-start | bytes 1572868
  7.2 44.3 %copy-start = (bf16[512,512]{1,0:T(8,128)(2,1)S(1)}, bf16[512,512]{1,0:T(8,128)(2,1)}, u32[]{:S(2)}) copy-start(bf16[512,512]{1,0:T(8,128)(2,1)} %param.13) | copy-start | bytes 1572868
  7.2 42.7 %all-gather.3.cloned.1.call-start = ((), (), s32[]{:S(2)}) async-start(), calls=%async_computation | async-start | bytes 1327104 | tf_op jit(solution)/shard_map/all_gather | solution.py:119
  7.9 236.6 %all-reduce.4.cloned.1.call-start = ((), (), s32[]{:S(2)}) async-start(), calls=%async_computation.1 | async-start | bytes 655360 | tf_op jit(solution)/shard_map/psum | solution.py:153
  51.5 1.9 copy-start.2
  55.3 1.9 copy-start.2
  68.5 13.9 %collective-permute-start = (f32[128,1088]{0,1:T(8,128)}, f32[128,1088]{0,1:T(8,128)S(1)}, u32[]{:S(2)}, u32[]{:S(2)}) collective-permute-start(f32[128,1088]{0,1:T(8,128)} %maximum_add_fusion.3), channel_id=1, source_target_pairs={{0,4},{4,8},{8,12},{12,16},{16,20},{20,24},{24,28},{28,0},{1,5},{5... | collective-permute-start | bytes 1671176 | tf_op jit(solution)/shard_map/while/body/eval_jaxpr/ppermute | solution.py:20
  87.9 13.0 %collective-permute-start = (f32[128,1088]{0,1:T(8,128)}, f32[128,1088]{0,1:T(8,128)S(1)}, u32[]{:S(2)}, u32[]{:S(2)}) collective-permute-start(f32[128,1088]{0,1:T(8,128)} %maximum_add_fusion.3), channel_id=1, source_target_pairs={{0,4},{4,8},{8,12},{12,16},{16,20},{20,24},{24,28},{28,0},{1,5},{5... | collective-permute-start | bytes 1671176 | tf_op jit(solution)/shard_map/while/body/eval_jaxpr/ppermute | solution.py:20
  106.4 12.2 %collective-permute-start = (f32[128,1088]{0,1:T(8,128)}, f32[128,1088]{0,1:T(8,128)S(1)}, u32[]{:S(2)}, u32[]{:S(2)}) collective-permute-start(f32[128,1088]{0,1:T(8,128)} %maximum_add_fusion.3), channel_id=1, source_target_pairs={{0,4},{4,8},{8,12},{12,16},{16,20},{20,24},{24,28},{28,0},{1,5},{5... | collective-permute-start | bytes 1671176 | tf_op jit(solution)/shard_map/while/body/eval_jaxpr/ppermute | solution.py:20
  124.1 11.3 %collective-permute-start = (f32[128,1088]{0,1:T(8,128)}, f32[128,1088]{0,1:T(8,128)S(1)}, u32[]{:S(2)}, u32[]{:S(2)}) collective-permute-start(f32[128,1088]{0,1:T(8,128)} %maximum_add_fusion.3), channel_id=1, source_target_pairs={{0,4},{4,8},{8,12},{12,16},{16,20},{20,24},{24,28},{28,0},{1,5},{5... | collective-permute-start | bytes 1671176 | tf_op jit(solution)/shard_map/while/body/eval_jaxpr/ppermute | solution.py:20
  140.9 10.5 %collective-permute-start = (f32[128,1088]{0,1:T(8,128)}, f32[128,1088]{0,1:T(8,128)S(1)}, u32[]{:S(2)}, u32[]{:S(2)}) collective-permute-start(f32[128,1088]{0,1:T(8,128)} %maximum_add_fusion.3), channel_id=1, source_target_pairs={{0,4},{4,8},{8,12},{12,16},{16,20},{20,24},{24,28},{28,0},{1,5},{5... | collective-permute-start | bytes 1671176 | tf_op jit(solution)/shard_map/while/body/eval_jaxpr/ppermute | solution.py:20
  156.8 9.5 %collective-permute-start = (f32[128,1088]{0,1:T(8,128)}, f32[128,1088]{0,1:T(8,128)S(1)}, u32[]{:S(2)}, u32[]{:S(2)}) collective-permute-start(f32[128,1088]{0,1:T(8,128)} %maximum_add_fusion.3), channel_id=1, source_target_pairs={{0,4},{4,8},{8,12},{12,16},{16,20},{20,24},{24,28},{28,0},{1,5},{5... | collective-permute-start | bytes 1671176 | tf_op jit(solution)/shard_map/while/body/eval_jaxpr/ppermute | solution.py:20
  171.8 9.5 %collective-permute-start = (f32[128,1088]{0,1:T(8,128)}, f32[128,1088]{0,1:T(8,128)S(1)}, u32[]{:S(2)}, u32[]{:S(2)}) collective-permute-start(f32[128,1088]{0,1:T(8,128)} %maximum_add_fusion.3), channel_id=1, source_target_pairs={{0,4},{4,8},{8,12},{12,16},{16,20},{20,24},{24,28},{28,0},{1,5},{5... | collective-permute-start | bytes 1671176 | tf_op jit(solution)/shard_map/while/body/eval_jaxpr/ppermute | solution.py:20
  182.3 12.3 %collective-permute-start.1 = (f32[128,1088]{0,1:T(8,128)S(1)}, f32[128,1088]{0,1:T(8,128)S(1)}, u32[]{:S(2)}, u32[]{:S(2)}) collective-permute-start(f32[128,1088]{0,1:T(8,128)S(1)} %maximum_add_fusion.1), channel_id=1, source_target_pairs={{0,4},{4,8},{8,12},{12,16},{16,20},{20,24},{24,28},{28,0},{1,5},{5... | collective-permute-start | bytes 1671176 | tf_op jit(solution)/shard_map/ppermute | solution.py:20
  195.4 1.6 copy-start.3
  196.9 154.5 %all-reduce.6.cloned.1.call-start = ((), (), s32[]{:S(2)}) async-start(), calls=%async_computation.2 | async-start | bytes 4194304 | tf_op jit(solution)/shard_map/psum | solution.py:158
  351.3 2.6 copy-start.4
Sparse Core Ops, SparseCore 0:
  10.1 39.8 all-gather.2
  197.0 47.4 all-reduce.3
  248.8 102.5 all-reduce.5
where the time goes:
time: 366 us; the launch traced here: 362 us
  waiting for transfers between devices  259 us (71%)
  matrix products  54.4 us (15%)
  between operations  14.1 us (4%)
  blocking collectives  11.9 us (3%)
  other arithmetic  11.5 us (3%)
  local copies, waits for them, and re-layouts  10.1 us (3%)
    psum x1, waiting for transfers between devices, shards(): key_up_grad, value_up_grad = lax.psum((key_term, value_term), 'seq')  105 us
    ppermute x8, waiting for transfers between devices, shifted(): return lax.ppermute(value, axis, pairs)  83.5 us
    psum x1, waiting for transfers between devices, shards(): latent_grad = lax.psum(latent_part, 'head')  42.3 us
    all_gather x1, waiting for transfers between devices, shards(): gathered = lax.all_gather(latents, 'seq', axis=0, tiled=True)  27 us
    dot_general x10, matrix products, up_project(): jnp.dot(compressed, value_up, preferred_element_type=jnp.float32)  12.5 us
    all_gather x1, blocking collectives, shards(): every_pos = lax.all_gather(positions, 'seq', axis=0, tiled=True)  11.9 us
    dot_general x10, matrix products, up_project(): jnp.dot(compressed, key_up, preferred_element_type=jnp.float32)  10.4 us
    dot_general x10, matrix products, scores_of(): jnp.einsum('bhd,kd->hbk', q_rope, rope_keys, preferred_element_type=jnp.f...  8.12 us
  transfers between devices with their start and end apart: 11, of which 11 were waited for; matrix products, arithmetic and copies ran while one was open for 5% of the time, Pallas kernels for 0%

commit v1 on v0

v1 whole, which is shorter than its diff:
```python
import itertools
import math

import jax
import jax.numpy as jnp
from jax import lax
from jax.experimental import pallas as pl
from jax.experimental.pallas import tpu as pltpu
from jax.sharding import PartitionSpec as P

D_LAT = 512
D_ROPE = 64
D_NOPE = 128
D_V = 128
D_QK = D_NOPE + D_ROPE
LANE = 128
NEG = -1e30
MESH = pl.DeviceIdType.MESH
F32 = jnp.float32
BF16 = jnp.bfloat16


def bit(index, b):
    return (index // (1 << b)) % 2


def flip(index, b):
    return index + (1 << b) * (1 - 2 * bit(index, b))


def with_bits(index, bits, values):
    for b, value in zip(bits, values):
        index = index + (1 << b) * (value - bit(index, b))
    return index


def choices(bits):
    return list(itertools.product((0, 1), repeat=len(bits)))


def nn(a, b):
    return lax.dot_general(a, b, (((1,), (0,)), ((), ())), preferred_element_type=F32)


def nt(a, b):
    return lax.dot_general(a, b, (((1,), (1,)), ((), ())), preferred_element_type=F32)


def tn(a, b):
    return lax.dot_general(a, b, (((0,), (0,)), ((), ())), preferred_element_type=F32)


class Sems:
    def __init__(self, send, recv):
        self.send, self.recv, self.used = send, recv, 0
        self.sent = []

    def copy(self, src, dst, device):
        k = self.used
        self.used += 1
        copy = pltpu.make_async_remote_copy(
            src_ref=src,
            dst_ref=dst,
            send_sem=self.send.at[k],
            recv_sem=self.recv.at[k],
            device_id=device,
            device_id_type=MESH,
        )
        copy.start()
        self.sent.append(copy)
        return copy


def reduce_steps(sems, me, order, device_of, part, slots):
    slot = 0
    for k, b in enumerate(order):
        rest = order[k + 1 :]
        copies = []
        for values in choices(rest):
            leaving = with_bits(flip(me, b), rest, values)
            copies.append((sems.copy(part(leaving), slots.at[slot], device_of(flip(me, b))), slot, values))
            slot += 1
        yield
        for copy, at, values in copies:
            copy.wait_recv()
            kept = part(with_bits(me, rest, values))
            kept[...] = (kept[...].astype(F32) + slots[at].astype(F32)).astype(BF16)


def gather_steps(sems, me, order, device_of, part):
    for k, b in enumerate(order):
        done = order[:k]
        copies = []
        for values in choices(done):
            held = with_bits(me, done, values)
            copies.append(sems.copy(part(held), part(held), device_of(flip(me, b))))
        yield
        for copy in copies:
            copy.wait_recv()


def kernel(
    nseq, nhead,
    q_ref, lat_ref, ku_ref, vu_ref, do_ref, pos_ref,
    dq_ref, dl_ref, dk_ref, dv_ref,
    lat, kk, vv, sc, dp, top, kv, rope, gk, gv, fk, fv, rk, rv, lb, rh, rl, fl, dqs,
    send, recv,
):
    seq, head = lax.axis_index("seq"), lax.axis_index("head")
    seq_bits = list(range(nseq.bit_length() - 1))
    head_bits = list(range(nhead.bit_length() - 1))
    rows = lat_ref.shape[0]
    half = rows // 2
    heads = ku_ref.shape[1] // D_NOPE
    qrows = q_ref.shape[0]
    scale = 1.0 / math.sqrt(D_QK)
    sems = Sems(send, recv)

    def on_seq(s):
        return (s, head)

    def on_head(h):
        return (seq, h)

    barrier = pltpu.get_barrier_semaphore()
    for b in seq_bits:
        pl.semaphore_signal(barrier, inc=1, device_id=on_seq(flip(seq, b)), device_id_type=MESH)
    for b in head_bits:
        pl.semaphore_signal(barrier, inc=1, device_id=on_head(flip(head, b)), device_id_type=MESH)
    pl.semaphore_wait(barrier, len(seq_bits) + len(head_bits))

    core = bit(head, 0)
    other = on_head(flip(head, 0))
    top[...] = jnp.full(top.shape, NEG, F32)

    def mine_of(part):
        return lat.at[pl.ds(pl.multiple_of(part * rows + core * half, half), half)]

    def at_rows(part):
        return pl.ds(pl.multiple_of(part * rows, rows), rows)

    def take(part):
        here = at_rows(part)
        block = lat[here, :]
        comp = block[:, :D_LAT]
        keys = nn(comp, ku_ref[...]).astype(BF16)
        vals = nn(comp, vu_ref[...]).astype(BF16)
        kk[here, :] = keys
        vv[here, :] = vals
        kpos = block[:, D_LAT + D_ROPE :].astype(F32)
        kpos = kpos[:, 0:1] * float(LANE) + kpos[:, 1:2]
        visible = kpos <= pos_ref[...]
        rkeys = block[:, D_LAT : D_LAT + D_ROPE]
        for h in range(heads):
            qn = q_ref[:, h * D_QK : h * D_QK + D_NOPE]
            qr = q_ref[:, h * D_QK + D_NOPE : (h + 1) * D_QK]
            s = nt(keys[:, h * D_NOPE : (h + 1) * D_NOPE], qn) + nt(rkeys, qr)
            s = jnp.where(visible, s * scale, NEG)
            sc[h, here, :] = s
            top[h : h + 1, :] = jnp.maximum(top[h : h + 1, :], jnp.max(s, axis=0, keepdims=True))
            dp[h, here, :] = nt(vals[:, h * D_V : (h + 1) * D_V], do_ref[:, h * D_V : (h + 1) * D_V])

    order = seq_bits[::-1]
    lat[at_rows(seq), :] = lat_ref[...]
    own_half = lat_ref.at[pl.ds(pl.multiple_of(core * half, half), half)]
    fresh = [seq]
    for k, b in enumerate(order):
        copies, parts = [], []
        for values in choices(order[:k]):
            held = with_bits(seq, order[:k], values)
            src = own_half if not any(True for _ in order[:k]) else mine_of(held)
            copies.append(sems.copy(src, mine_of(held), on_seq(flip(seq, b))))
            parts.append(with_bits(flip(seq, b), order[:k], values))
        for part in fresh:
            take(part)
        passed = []
        for copy, part in zip(copies, parts):
            copy.wait_recv()
            passed.append(sems.copy(mine_of(part), mine_of(part), other))
        for copy in passed:
            copy.wait_recv()
        fresh = parts
    for part in fresh:
        take(part)

    tile = math.gcd(lat.shape[0], 256)
    tiles = lat.shape[0] // tile

    def sums(t, carry):
        here = pl.ds(pl.multiple_of(t * tile, tile), tile)
        out = []
        for h in range(heads):
            total, weighted = carry[h]
            p = jnp.exp(sc[h, here, :] - top[h : h + 1, :])
            sc[h, here, :] = p
            total = total + jnp.sum(p, axis=0, keepdims=True)
            weighted = weighted + jnp.sum(p * dp[h, here, :], axis=0, keepdims=True)
            out.append((total, weighted))
        return tuple(out)

    zero = jnp.zeros((1, qrows), F32)
    stats = lax.fori_loop(0, tiles, sums, tuple((zero, zero) for _ in range(heads)))
    inv = [1.0 / total for total, _ in stats]
    delta = [weighted / total for total, weighted in stats]
    dqs[...] = jnp.zeros(dqs.shape, F32)

    def grads(t, carry):
        here = pl.ds(pl.multiple_of(t * tile, tile), tile)
        rkeys = lat[here, D_LAT : D_LAT + D_ROPE]
        rsum = jnp.zeros((tile, D_ROPE), F32)
        for h in range(heads):
            qn = q_ref[:, h * D_QK : h * D_QK + D_NOPE]
            qr = q_ref[:, h * D_QK + D_NOPE : (h + 1) * D_QK]
            prob = sc[h, here, :] * inv[h]
            ds = (prob * (dp[h, here, :] - delta[h]) * scale).astype(BF16)
            kv[here, h * D_NOPE : (h + 1) * D_NOPE] = nn(ds, qn).astype(BF16)
            at = heads * D_NOPE + h * D_V
            kv[here, at : at + D_V] = nn(prob.astype(BF16), do_ref[:, h * D_V : (h + 1) * D_V]).astype(BF16)
            rsum = rsum + nn(ds, qr)
            dqs[h, :, :D_NOPE] += tn(ds, kk[here, h * D_NOPE : (h + 1) * D_NOPE])
            dqs[h, :, D_NOPE:D_QK] += tn(ds, rkeys)
        rope[here, :] = rsum
        return carry

    lax.fori_loop(0, tiles, grads, 0)

    for c in range(D_LAT // LANE):
        up = tn(lat[:, c * LANE : (c + 1) * LANE], kv[...]).astype(BF16)
        gk[c * LANE : (c + 1) * LANE, :] = up[:, : heads * D_NOPE]
        gv[c * LANE : (c + 1) * LANE, :] = up[:, heads * D_NOPE :]

    share = D_LAT // nseq

    def rows_of(ref):
        return lambda part: ref.at[pl.ds(pl.multiple_of(part * share, share), share)]

    def both(source, final, slots, order):
        yield from reduce_steps(sems, seq, order, on_seq, rows_of(source), slots)
        done = rows_of(final)(seq)
        done[...] = rows_of(source)(seq)[...]
        yield from gather_steps(sems, seq, order[::-1], on_seq, rows_of(final))

    def latent_grads():
        sub = rows // nhead

        def fold(part, carry):
            here = at_rows(part)
            total = nt(kv[here, : heads * D_NOPE], ku_ref[...])
            total = total + nt(kv[here, heads * D_NOPE :], vu_ref[...])
            for a in range(nhead):
                cut = slice(a * sub, (a + 1) * sub)
                lb[a, part, :, :D_LAT] = total[cut].astype(BF16)
                lb[a, part, :, D_LAT : D_LAT + D_ROPE] = rope[
                    pl.ds(pl.multiple_of(part * rows + a * sub, sub), sub), :
                ].astype(BF16)
            return carry

        lb[:, :, :, D_LAT:] = jnp.zeros(lb.shape[:3] + (lb.shape[3] - D_LAT,), BF16)
        lax.fori_loop(0, nseq, fold, 0)
        yield from reduce_steps(sems, head, head_bits, on_head, lambda a: lb.at[a], rh)
        mine = lb.at[head]
        yield from reduce_steps(sems, seq, seq_bits, on_seq, lambda s: mine.at[s], rl)
        fl[head] = lb[head, seq]
        yield from gather_steps(sems, head, head_bits[::-1], on_head, lambda a: fl.at[a])

    pipes = [
        both(gv, fv, rv, seq_bits[1:] + seq_bits[:1]),
        both(gk, fk, rk, seq_bits),
        latent_grads(),
    ]
    first = True
    while pipes:
        left = []
        for pipe in pipes:
            try:
                next(pipe)
                left.append(pipe)
            except StopIteration:
                pass
        pipes = left
        if first:
            first = False
            for h in range(heads):
                dq_ref[:, h * D_QK : (h + 1) * D_QK] = dqs[h, :, :D_QK].astype(BF16)
    dk_ref[...] = fk[...].astype(F32)
    dv_ref[...] = fv[...].astype(F32)
    sub = rows // nhead
    for a in range(nhead):
        dl_ref[a * sub : (a + 1) * sub, :] = fl[a, :, : D_LAT + D_ROPE].astype(F32)
    for copy in sems.sent:
        copy.wait_send()


def make_shards(nseq, nhead):
    def shards(queries, latents, key_up, value_up, out_grad, positions):
        rows, heads = latents.shape[0], key_up.shape[1] // D_NOPE
        qrows = queries.shape[0]
        count = rows * nseq
        width = -(-(D_LAT + D_ROPE + 2) // LANE) * LANE
        high, low = positions // LANE, positions % LANE
        coded = jnp.stack([high, low], axis=1).astype(BF16)
        packed = jnp.concatenate(
            [latents, coded, jnp.zeros((rows, width - D_LAT - D_ROPE - 2), BF16)], axis=1
        )
        qpos = positions.astype(F32)[None, :]
        up_cols = heads * D_NOPE
        share = D_LAT // nseq
        sub = rows // nhead
        copies = 6 * (nseq - 1) + (nseq - 1) + 2 * (nhead - 1)
        vmem = pl.BlockSpec(memory_space=pltpu.VMEM)
        body = lambda *refs: kernel(nseq, nhead, *refs)
        return pl.pallas_call(
            body,
            out_shape=(
                jax.ShapeDtypeStruct(queries.shape, BF16),
                jax.ShapeDtypeStruct(latents.shape, F32),
                jax.ShapeDtypeStruct(key_up.shape, F32),
                jax.ShapeDtypeStruct(value_up.shape, F32),
            ),
            in_specs=[vmem] * 6,
            out_specs=(vmem,) * 4,
            scratch_shapes=[
                pltpu.VMEM((count, width), BF16),
                pltpu.VMEM((count, up_cols), BF16),
                pltpu.VMEM((count, up_cols), BF16),
                pltpu.VMEM((heads, count, qrows), F32),
                pltpu.VMEM((heads, count, qrows), F32),
                pltpu.VMEM((heads, qrows), F32),
                pltpu.VMEM((count, 2 * up_cols), BF16),
                pltpu.VMEM((count, D_ROPE), F32),
                pltpu.VMEM((D_LAT, up_cols), BF16),
                pltpu.VMEM((D_LAT, up_cols), BF16),
                pltpu.VMEM((D_LAT, up_cols), BF16),
                pltpu.VMEM((D_LAT, up_cols), BF16),
                pltpu.VMEM((nseq - 1, share, up_cols), BF16),
                pltpu.VMEM((nseq - 1, share, up_cols), BF16),
                pltpu.VMEM((nhead, nseq, sub, width), BF16),
                pltpu.VMEM((nhead - 1, nseq, sub, width), BF16),
                pltpu.VMEM((nseq - 1, sub, width), BF16),
                pltpu.VMEM((nhead, sub, width), BF16),
                pltpu.VMEM((heads, qrows, 2 * LANE), F32),
                pltpu.SemaphoreType.DMA((copies,)),
                pltpu.SemaphoreType.DMA((copies,)),
            ],
            compiler_params=pltpu.CompilerParams(
                collective_id=0, has_side_effects=True, vmem_limit_bytes=60 * 1024 * 1024
            ),
        )(queries, packed, key_up, value_up, out_grad, qpos)

    return shards


def solution(mesh):
    in_specs = (
        P("seq", "head"),
        P("seq", None),
        P(None, "head"),
        P(None, "head"),
        P("seq", "head"),
        P("seq"),
    )
    out_specs = (P("seq", "head"), P("seq", None), P(None, "head"), P(None, "head"))
    shards = make_shards(mesh.shape["seq"], mesh.shape["head"])
    return jax.shard_map(shards, mesh=mesh, in_specs=in_specs, out_specs=out_specs, check_vma=False)
```

time: 366 us -> 88.2 us (0.24); the launches traced: 362 us -> 88 us
  waiting for transfers between devices: 259 us -> 0 us
  Pallas kernels: 0 us -> 78.2 us
  matrix products: 54.4 us -> 0 us
  between operations: 14.1 us -> 0.67 us
  blocking collectives: 11.9 us -> 0 us
  other arithmetic: 11.5 us -> 1.28 us
    psum x2 -> x0, waiting for transfers between devices: 147 us -> none  [the longest x1 105 us: shards(): key_up_grad, value_up_grad = lax.psum((key_term, value_term), 'seq')]
    ppermute x8 -> x0, waiting for transfers between devices: 83.5 us -> none  [shifted(): return lax.ppermute(value, axis, pairs)]
    pallas_call x0 -> x1, Pallas kernels: none -> 78.2 us  [shards(): pl.pallas_call(body, out_shape=(jax.ShapeDtypeStruct(queries.shape, BF16)...]
    dot_general x94 -> x0, matrix products: 54.4 us -> none  [the longest x10 12.5 us: up_project(): jnp.dot(compressed, value_up, preferred_element_type=jnp.float32)]
    all_gather x1 -> x0, waiting for transfers between devices: 27 us -> none  [shards(): gathered = lax.all_gather(latents, 'seq', axis=0, tiled=True)]
    all_gather x1 -> x0, blocking collectives: 11.9 us -> none  [shards(): every_pos = lax.all_gather(positions, 'seq', axis=0, tiled=True)]
    add x17 -> x0, other arithmetic: 7.65 us -> none  [the longest x15 7.62 us: grad_block(): return (grads + part, q_acc + q_grad)]
    unnamed x18 -> x10, local copies, waits for them, and re-layouts: 8 us -> 5.64 us
  transfers between devices with their start and end apart: 11 -> 0, of which waited for: 11 -> 0; matrix products, arithmetic and copies ran while one was open for 5% -> 0% of each run, Pallas kernels for 0% -> 0%
where the time goes in v1:
time: 88.2 us; the launch traced here: 88 us
  Pallas kernels  78.2 us (89%)
  local copies, waits for them, and re-layouts  7.87 us (9%)
  other arithmetic  1.28 us (1%)
    pallas_call x1, Pallas kernels, shards(): pl.pallas_call(body, out_shape=(jax.ShapeDtypeStruct(queries.shape, BF16)...  78.2 us
    unnamed x10, local copies, waits for them, and re-layouts  5.64 us
    pallas_call x1, local copies, waits for them, and re-layouts, shards(): pl.pallas_call(body, out_shape=(jax.ShapeDtypeStruct(queries.shape, BF16)...  1.88 us

profile of v1, /device:TPU:17, one launch (start us, length us, event | category | flops | bytes accessed | tf_op | source)
XLA Modules:
  0.0 88.0 jit_solution(12508766466813972434)
XLA Ops:
  0.6 0.0 copy-start.2
  0.7 0.1 pad.3.clone
  0.7 0.6 copy-done.2
  1.3 0.5 convert_bitcast_fusion
  1.8 0.1 copy.11
  1.9 0.1 copy.12
  2.1 1.1 %copy.10 = bf16[128,576]{1,0:T(8,128)(2,1)S(1)} copy(bf16[128,576]{0,1:T(8,128)(2,1)} %param.7) | data formatting | bytes 294912 | tf_op args[1]
  3.1 0.8 maximum_maximum_fusion.refs_1_
  3.9 78.2 %shard_map.93 = (bf16[128,768]{1,0:T(8,128)(2,1)}, f32[128,576]{1,0:T(8,128)}, f32[512,512]{1,0:T(8,128)}, f32[512,512]{1,0:T(8,128)}) custom-call(bf16[128,768]{1,0:T(8,128)(2,1)} %refs_0_.1, bf16[128,640]{1,0:T(8,128)(2,1)} %maximum_maximum_fusion.refs_1_, bf16[512,512]{1,0:T(8,128)(2,1)} %refs_2_.1, bf16[512,512]{1,0:T(8,128)(2,1)} %refs_3_.1, ...), custom_call_target="tpu_custom_call" | custom-call | tf_op jit(solution)/shard_map/pallas_call | solution.py:312
  82.1 0.0 copy-start.1
  82.1 1.9 %copy.13 = f32[128,576]{0,1:T(8,128)} copy(f32[128,576]{1,0:T(8,128)} %get-tuple-element.5) | data formatting | bytes 589824 | tf_op jit(solution)/shard_map/pallas_call | solution.py:312
  84.0 0.0 copy-done.1
  84.0 0.7 copy.17
  84.6 0.0 copy-start
  84.6 2.4 %copy.18 = f32[512,512]{1,0:T(8,128)} copy(f32[512,512]{1,0:T(8,128)} %get-tuple-element.17) | data formatting | bytes 2097152
  87.0 0.0 copy-done
  87.0 1.0 %copy.19 = f32[512,512]{1,0:T(8,128)} copy(f32[512,512]{1,0:T(8,128)S(1)} %copy-done) | data formatting | bytes 2097152
  (1 shorter events, 0.0 us)
Async XLA Ops:
  0.6 0.7 copy-start.2
  82.1 1.9 %copy-start.1 = (bf16[128,768]{1,0:T(8,128)(2,1)S(1)}, bf16[128,768]{1,0:T(8,128)(2,1)}, u32[]{:S(2)}) copy-start(bf16[128,768]{1,0:T(8,128)(2,1)} %get-tuple-element.15) | copy-start | bytes 589828
  84.6 2.4 %copy-start = (f32[512,512]{1,0:T(8,128)S(1)}, f32[512,512]{1,0:T(8,128)}, u32[]{:S(2)}) copy-start(f32[512,512]{1,0:T(8,128)} %get-tuple-element.18) | copy-start | bytes 3145732

commit v2 on v1

--- a/solution.py
+++ b/solution.py
@@ -78,13 +78,13 @@
         copies = []
         for values in choices(rest):
             leaving = with_bits(flip(me, b), rest, values)
-            copies.append((sems.copy(part(leaving), slots.at[slot], device_of(flip(me, b))), slot, values))
+            copies.append((sems.copy(part(leaving), slots(slot), device_of(flip(me, b))), slot, values))
             slot += 1
         yield
         for copy, at, values in copies:
             copy.wait_recv()
             kept = part(with_bits(me, rest, values))
-            kept[...] = (kept[...].astype(F32) + slots[at].astype(F32)).astype(BF16)
+            kept[...] = (kept[...].astype(F32) + slots(at)[...].astype(F32)).astype(BF16)
 
 
 def gather_steps(sems, me, order, device_of, part):
@@ -132,9 +132,6 @@
     core = bit(head, 0)
     other = on_head(flip(head, 0))
     top[...] = jnp.full(top.shape, NEG, F32)
-
-    def mine_of(part):
-        return lat.at[pl.ds(pl.multiple_of(part * rows + core * half, half), half)]
 
     def at_rows(part):
         return pl.ds(pl.multiple_of(part * rows, rows), rows)
@@ -160,28 +157,63 @@
             top[h : h + 1, :] = jnp.maximum(top[h : h + 1, :], jnp.max(s, axis=0, keepdims=True))
             dp[h, here, :] = nt(vals[:, h * D_V : (h + 1) * D_V], do_ref[:, h * D_V : (h + 1) * D_V])
 
-    order = seq_bits[::-1]
+    piece = half // 2
+    down = seq_bits[::-1]
+    orders = [down, down[:-2] + down[-2:][::-1]]
     lat[at_rows(seq), :] = lat_ref[...]
-    own_half = lat_ref.at[pl.ds(pl.multiple_of(core * half, half), half)]
-    fresh = [seq]
-    for k, b in enumerate(order):
-        copies, parts = [], []
-        for values in choices(order[:k]):
-            held = with_bits(seq, order[:k], values)
-            src = own_half if not any(True for _ in order[:k]) else mine_of(held)
-            copies.append(sems.copy(src, mine_of(held), on_seq(flip(seq, b))))
-            parts.append(with_bits(flip(seq, b), order[:k], values))
+
+    def piece_of(part, p):
+        start = part * rows + core * half + p * piece
+        return lat.at[pl.ds(pl.multiple_of(start, piece), piece)]
+
+    def bring(p, order):
+        own = lat_ref.at[pl.ds(pl.multiple_of(core * half + p * piece, piece), piece)]
+        for k, b in enumerate(order):
+            copies = []
+            for values in choices(order[:k]):
+                held = with_bits(seq, order[:k], values)
+                src = own if k == 0 else piece_of(held, p)
+                part = with_bits(flip(seq, b), order[:k], values)
+                copies.append((sems.copy(src, piece_of(held, p), on_seq(flip(seq, b))), part))
+            yield None
+            passed = []
+            for copy, part in copies:
+                copy.wait_recv()
+                passed.append(sems.copy(piece_of(part, p), piece_of(part, p), other))
+            yield passed
+
+    brings = [bring(p, order) for p, order in enumerate(orders)]
+    for g in brings:
+        next(g)
+    common = max(len(down) - 2, 0)
+    fresh, waiting = [seq], []
+    for k in range(len(down)):
+        passed = []
+        for g in brings:
+            passed += next(g)
+            next(g, None)
         for part in fresh:
             take(part)
-        passed = []
-        for copy, part in zip(copies, parts):
-            copy.wait_recv()
-            passed.append(sems.copy(mine_of(part), mine_of(part), other))
-        for copy in passed:
-            copy.wait_recv()
-        fresh = parts
+        fresh = []
+        waiting += passed
+        if k < common:
+            for copy in waiting:
+                copy.wait_recv()
+            waiting = []
+            fresh = [with_bits(flip(seq, down[k]), down[:k], values) for values in choices(down[:k])]
     for part in fresh:
         take(part)
+    for copy in waiting:
+        copy.wait_recv()
+    tail = down[common:]
+    for late in choices(tail):
+        if not any(late):
+            continue
+        base = seq
+        for b, turned in zip(tail, late):
+            base = flip(base, b) if turned else base
+        for values in choices(down[:common]):
+            take(with_bits(base, down[:common], values))
 
     tile = math.gcd(lat.shape[0], 256)
     tiles = lat.shape[0] // tile
@@ -231,11 +263,17 @@
 
     share = D_LAT // nseq
 
-    def rows_of(ref):
-        return lambda part: ref.at[pl.ds(pl.multiple_of(part * share, share), share)]
-
-    def both(source, final, slots, order):
-        yield from reduce_steps(sems, seq, order, on_seq, rows_of(source), slots)
+    half_cols = heads * D_NOPE // 2
+
+    def both(source, final, slots, order, c):
+        cols = slice(c * half_cols, (c + 1) * half_cols)
+
+        def rows_of(ref):
+            return lambda part: ref.at[pl.ds(pl.multiple_of(part * share, share), share), cols]
+
+        yield from reduce_steps(
+            sems, seq, order, on_seq, rows_of(source), lambda k: slots.at[k, :, cols]
+        )
         done = rows_of(final)(seq)
         done[...] = rows_of(source)(seq)[...]
         yield from gather_steps(sems, seq, order[::-1], on_seq, rows_of(final))
@@ -257,15 +295,17 @@
 
         lb[:, :, :, D_LAT:] = jnp.zeros(lb.shape[:3] + (lb.shape[3] - D_LAT,), BF16)
         lax.fori_loop(0, nseq, fold, 0)
-        yield from reduce_steps(sems, head, head_bits, on_head, lambda a: lb.at[a], rh)
+        yield from reduce_steps(sems, head, head_bits, on_head, lambda a: lb.at[a], lambda k: rh.at[k])
         mine = lb.at[head]
-        yield from reduce_steps(sems, seq, seq_bits, on_seq, lambda s: mine.at[s], rl)
+        yield from reduce_steps(sems, seq, seq_bits, on_seq, lambda s: mine.at[s], lambda k: rl.at[k])
         fl[head] = lb[head, seq]
         yield from gather_steps(sems, head, head_bits[::-1], on_head, lambda a: fl.at[a])
 
     pipes = [
-        both(gv, fv, rv, seq_bits[1:] + seq_bits[:1]),
-        both(gk, fk, rk, seq_bits),
+        both(gv, fv, rv, seq_bits[1:] + seq_bits[:1], 0),
+        both(gk, fk, rk, seq_bits, 0),
+        both(gv, fv, rv, seq_bits[1:] + seq_bits[:1], 1),
+        both(gk, fk, rk, seq_bits, 1),
         latent_grads(),
     ]
     first = True
@@ -282,11 +322,11 @@
             first = False
             for h in range(heads):
                 dq_ref[:, h * D_QK : (h + 1) * D_QK] = dqs[h, :, :D_QK].astype(BF16)
-    dk_ref[...] = fk[...].astype(F32)
-    dv_ref[...] = fv[...].astype(F32)
+    dk_ref[...] = fk[...]
+    dv_ref[...] = fv[...]
     sub = rows // nhead
     for a in range(nhead):
-        dl_ref[a * sub : (a + 1) * sub, :] = fl[a, :, : D_LAT + D_ROPE].astype(F32)
+        dl_ref[a * sub : (a + 1) * sub, :] = fl[a, :, : D_LAT + D_ROPE]
     for copy in sems.sent:
         copy.wait_send()
 
@@ -306,16 +346,16 @@
         up_cols = heads * D_NOPE
         share = D_LAT // nseq
         sub = rows // nhead
-        copies = 6 * (nseq - 1) + (nseq - 1) + 2 * (nhead - 1)
+        copies = 4 * (nseq - 1) + 8 * (nseq - 1) + (nseq - 1) + 2 * (nhead - 1)
         vmem = pl.BlockSpec(memory_space=pltpu.VMEM)
         body = lambda *refs: kernel(nseq, nhead, *refs)
-        return pl.pallas_call(
+        dq, dl, dk, dv = pl.pallas_call(
             body,
             out_shape=(
                 jax.ShapeDtypeStruct(queries.shape, BF16),
-                jax.ShapeDtypeStruct(latents.shape, F32),
-                jax.ShapeDtypeStruct(key_up.shape, F32),
-                jax.ShapeDtypeStruct(value_up.shape, F32),
+                jax.ShapeDtypeStruct(latents.shape, BF16),
+                jax.ShapeDtypeStruct(key_up.shape, BF16),
+                jax.ShapeDtypeStruct(value_up.shape, BF16),
             ),
             in_specs=[vmem] * 6,
             out_specs=(vmem,) * 4,
@@ -346,6 +386,7 @@
                 collective_id=0, has_side_effects=True, vmem_limit_bytes=60 * 1024 * 1024
             ),
         )(queries, packed, key_up, value_up, out_grad, qpos)
+        return dq, dl.astype(F32), dk.astype(F32), dv.astype(F32)
 
     return shards
 

time: 88.2 us -> 77.9 us (0.88)
  Pallas kernels: 78.2 us -> 68.2 us
  local copies, waits for them, and re-layouts: 7.87 us -> 3.02 us
  other arithmetic: 1.28 us -> 5.31 us
    pallas_call x1, Pallas kernels: 78.2 us -> 68.2 us  [shards(): pl.pallas_call(body, out_shape=(jax.ShapeDtypeStruct(queries.shape, BF16)...]
    convert_element_type x0 -> x2, other arithmetic: none -> 3.3 us  [shards(): return (dq, dl.astype(F32), dk.astype(F32), dv.astype(F32))]
    unnamed x10 -> x9, local copies, waits for them, and re-layouts: 5.64 us -> 2.67 us
    pallas_call x1 -> x0, local copies, waits for them, and re-layouts: 1.88 us -> none  [shards(): pl.pallas_call(body, out_shape=(jax.ShapeDtypeStruct(queries.shape, BF16)...]
where the time goes in v2:
time: 77.9 us; the launch traced here: 77.1 us
  Pallas kernels  68.2 us (88%)
  other arithmetic  5.31 us (7%)
  local copies, waits for them, and re-layouts  3.02 us (4%)
    pallas_call x1, Pallas kernels, shards(): pl.pallas_call(body, out_shape=(jax.ShapeDtypeStruct(queries.shape, BF16)...  68.2 us
    convert_element_type x2, other arithmetic, shards(): return (dq, dl.astype(F32), dk.astype(F32), dv.astype(F32))  3.3 us
    unnamed x9, local copies, waits for them, and re-layouts  2.67 us

profile of v2, /device:TPU:17, one launch (start us, length us, event | category | flops | bytes accessed | tf_op | source)
XLA Modules:
  0.0 77.1 jit_solution(15204154763870282477)
XLA Ops:
  0.6 1.2 %convert_bitcast_fusion = (f32[1,128]{1,0:T(1,128)}, bf16[128,1]{0,1:T(2,128)(2,1)S(1)}, bf16[128,1]{0,1:T(2,128)(2,1)S(1)}) fusion(s32[128]{0:T(128)} %param.11), kind=kLoop, calls=%fused_computation.8 | loop fusion | flops 2816 | bytes 1536 | tf_op jit(solution)/shard_map/broadcast_in_dim | solution.py:345
  1.9 0.1 copy.11
  2.0 0.1 copy.12
  2.1 1.1 %copy.10 = bf16[128,576]{1,0:T(8,128)(2,1)S(1)} copy(bf16[128,576]{0,1:T(8,128)(2,1)} %param.7) | data formatting | bytes 294912 | tf_op args[1]
  3.2 0.1 pad.3.clone
  3.3 0.8 maximum_maximum_fusion.refs_1_
  4.1 68.2 %shard_map.93 = (bf16[128,768]{1,0:T(8,128)(2,1)}, bf16[128,576]{1,0:T(8,128)(2,1)}, bf16[512,512]{1,0:T(8,128)(2,1)}, bf16[512,512]{1,0:T(8,128)(2,1)}) custom-call(bf16[128,768]{1,0:T(8,128)(2,1)} %refs_0_.1, bf16[128,640]{1,0:T(8,128)(2,1)} %maximum_maximum_fusion.refs_1_, bf16[512,512]{1,0:T(8,128)(2,1)} %refs_2_.1, bf16[512,512]{1,0:T(8,128)(2,1)} %refs_3_.1, ...), custom_call_target="tpu_custom_call" | custom-call | tf_op jit(solution)/shard_map/pallas_call | solution.py:352
  72.2 0.0 copy-start
  72.2 2.2 %convert_element_type.15 = f32[512,512]{1,0:T(8,128)} convert(bf16[512,512]{1,0:T(8,128)(2,1)} %get-tuple-element.10) | non-fusion elementwise | flops 262144 | bytes 1572864 | tf_op jit(solution)/shard_map/convert_element_type | solution.py:389
  74.4 0.0 copy-done
  74.4 0.0 copy-start.2
  74.4 1.1 %convert_element_type.16 = f32[512,512]{1,0:T(8,128)} convert(bf16[512,512]{1,0:T(8,128)(2,1)S(1)} %copy-done) | non-fusion elementwise | flops 262144 | bytes 1572864 | tf_op jit(solution)/shard_map/convert_element_type | solution.py:389
  75.5 0.0 copy-done.2
  75.5 0.0 copy-start.1
  75.5 0.8 %copy.13 = f32[128,576]{0,1:T(8,128)} copy(bf16[128,576]{1,0:T(8,128)(2,1)S(1)} %copy-done.2) | data formatting | bytes 442368
  76.4 0.1 copy-done.1
  76.5 0.7 copy.15
  (1 shorter events, 0.0 us)
Async XLA Ops:
  72.2 2.2 %copy-start = (bf16[512,512]{1,0:T(8,128)(2,1)S(1)}, bf16[512,512]{1,0:T(8,128)(2,1)}, u32[]{:S(2)}) copy-start(bf16[512,512]{1,0:T(8,128)(2,1)} %get-tuple-element.11) | copy-start | bytes 1572868
  74.4 1.1 %copy-start.2 = (bf16[128,576]{1,0:T(8,128)(2,1)S(1)}, bf16[128,576]{1,0:T(8,128)(2,1)}, u32[]{:S(2)}) copy-start(bf16[128,576]{1,0:T(8,128)(2,1)} %get-tuple-element.9) | copy-start | bytes 442372
  75.5 0.9 %copy-start.1 = (bf16[128,768]{1,0:T(8,128)(2,1)S(1)}, bf16[128,768]{1,0:T(8,128)(2,1)}, u32[]{:S(2)}) copy-start(bf16[128,768]{1,0:T(8,128)(2,1)} %get-tuple-element.23) | copy-start | bytes 589828

commit v3 on v2

--- a/solution.py
+++ b/solution.py
@@ -263,10 +263,11 @@
 
     share = D_LAT // nseq
 
-    half_cols = heads * D_NOPE // 2
+    pieces = heads
+    width = heads * D_NOPE // pieces
 
     def both(source, final, slots, order, c):
-        cols = slice(c * half_cols, (c + 1) * half_cols)
+        cols = slice(c * width, (c + 1) * width)
 
         def rows_of(ref):
             return lambda part: ref.at[pl.ds(pl.multiple_of(part * share, share), share), cols]
@@ -302,12 +303,11 @@
         yield from gather_steps(sems, head, head_bits[::-1], on_head, lambda a: fl.at[a])
 
     pipes = [
-        both(gv, fv, rv, seq_bits[1:] + seq_bits[:1], 0),
-        both(gk, fk, rk, seq_bits, 0),
-        both(gv, fv, rv, seq_bits[1:] + seq_bits[:1], 1),
-        both(gk, fk, rk, seq_bits, 1),
         latent_grads(),
     ]
+    for c in reversed(range(pieces)):
+        pipes.insert(0, both(gk, fk, rk, seq_bits, c))
+        pipes.insert(0, both(gv, fv, rv, seq_bits[1:] + seq_bits[:1], c))
     first = True
     while pipes:
         left = []
@@ -346,7 +346,7 @@
         up_cols = heads * D_NOPE
         share = D_LAT // nseq
         sub = rows // nhead
-        copies = 4 * (nseq - 1) + 8 * (nseq - 1) + (nseq - 1) + 2 * (nhead - 1)
+        copies = 4 * (nseq - 1) + 4 * heads * (nseq - 1) + (nseq - 1) + 2 * (nhead - 1)
         vmem = pl.BlockSpec(memory_space=pltpu.VMEM)
         body = lambda *refs: kernel(nseq, nhead, *refs)
         dq, dl, dk, dv = pl.pallas_call(

time: 77.9 us -> 79 us (1.014)
  Pallas kernels: 68.2 us -> 69.5 us
    pallas_call x1, Pallas kernels: 68.2 us -> 69.5 us  [shards(): pl.pallas_call(body, out_shape=(jax.ShapeDtypeStruct(queries.shape, BF16)...]
where the time goes in v3:
time: 79 us; the launch traced here: 78.5 us
  Pallas kernels  69.5 us (88%)
  other arithmetic  5.31 us (7%)
  local copies, waits for them, and re-layouts  3.02 us (4%)
    pallas_call x1, Pallas kernels, shards(): pl.pallas_call(body, out_shape=(jax.ShapeDtypeStruct(queries.shape, BF16)...  69.5 us
    convert_element_type x2, other arithmetic, shards(): return (dq, dl.astype(F32), dk.astype(F32), dv.astype(F32))  3.3 us
    unnamed x9, local copies, waits for them, and re-layouts  2.67 us

profile of v3, /device:TPU:17, one launch (start us, length us, event | category | flops | bytes accessed | tf_op | source)
XLA Modules:
  0.0 78.5 jit_solution(3217803829820493383)
XLA Ops:
  0.6 1.2 %convert_bitcast_fusion = (f32[1,128]{1,0:T(1,128)}, bf16[128,1]{0,1:T(2,128)(2,1)S(1)}, bf16[128,1]{0,1:T(2,128)(2,1)S(1)}) fusion(s32[128]{0:T(128)} %param.11), kind=kLoop, calls=%fused_computation.8 | loop fusion | flops 2816 | bytes 1536 | tf_op jit(solution)/shard_map/broadcast_in_dim | solution.py:345
  1.9 0.1 copy.11
  2.0 0.1 copy.12
  2.1 1.1 %copy.10 = bf16[128,576]{1,0:T(8,128)(2,1)S(1)} copy(bf16[128,576]{0,1:T(8,128)(2,1)} %param.7) | data formatting | bytes 294912 | tf_op args[1]
  3.2 0.1 pad.3.clone
  3.3 0.8 maximum_maximum_fusion.refs_1_
  4.1 69.5 %shard_map.93 = (bf16[128,768]{1,0:T(8,128)(2,1)}, bf16[128,576]{1,0:T(8,128)(2,1)}, bf16[512,512]{1,0:T(8,128)(2,1)}, bf16[512,512]{1,0:T(8,128)(2,1)}) custom-call(bf16[128,768]{1,0:T(8,128)(2,1)} %refs_0_.1, bf16[128,640]{1,0:T(8,128)(2,1)} %maximum_maximum_fusion.refs_1_, bf16[512,512]{1,0:T(8,128)(2,1)} %refs_2_.1, bf16[512,512]{1,0:T(8,128)(2,1)} %refs_3_.1, ...), custom_call_target="tpu_custom_call" | custom-call | tf_op jit(solution)/shard_map/pallas_call | solution.py:352
  73.6 0.0 copy-start
  73.6 2.2 %convert_element_type.15 = f32[512,512]{1,0:T(8,128)} convert(bf16[512,512]{1,0:T(8,128)(2,1)} %get-tuple-element.10) | non-fusion elementwise | flops 262144 | bytes 1572864 | tf_op jit(solution)/shard_map/convert_element_type | solution.py:389
  75.8 0.0 copy-done
  75.8 0.0 copy-start.2
  75.8 1.1 %convert_element_type.16 = f32[512,512]{1,0:T(8,128)} convert(bf16[512,512]{1,0:T(8,128)(2,1)S(1)} %copy-done) | non-fusion elementwise | flops 262144 | bytes 1572864 | tf_op jit(solution)/shard_map/convert_element_type | solution.py:389
  76.9 0.0 copy-done.2
  76.9 0.0 copy-start.1
  76.9 0.8 %copy.13 = f32[128,576]{0,1:T(8,128)} copy(bf16[128,576]{1,0:T(8,128)(2,1)S(1)} %copy-done.2) | data formatting | bytes 442368
  77.7 0.1 copy-done.1
  77.8 0.7 copy.15
  (1 shorter events, 0.0 us)
Async XLA Ops:
  73.6 2.2 %copy-start = (bf16[512,512]{1,0:T(8,128)(2,1)S(1)}, bf16[512,512]{1,0:T(8,128)(2,1)}, u32[]{:S(2)}) copy-start(bf16[512,512]{1,0:T(8,128)(2,1)} %get-tuple-element.11) | copy-start | bytes 1572868
  75.8 1.1 %copy-start.2 = (bf16[128,576]{1,0:T(8,128)(2,1)S(1)}, bf16[128,576]{1,0:T(8,128)(2,1)}, u32[]{:S(2)}) copy-start(bf16[128,576]{1,0:T(8,128)(2,1)} %get-tuple-element.9) | copy-start | bytes 442372
  76.9 0.9 %copy-start.1 = (bf16[128,768]{1,0:T(8,128)(2,1)S(1)}, bf16[128,768]{1,0:T(8,128)(2,1)}, u32[]{:S(2)}) copy-start(bf16[128,768]{1,0:T(8,128)(2,1)} %get-tuple-element.23) | copy-start | bytes 589828
